TPU v7x, 32 devices: a whole 2x2x4 slice. The times are simulated.
32 devices in a mesh: grp: 8 (over z, y), mem: 4 (over x, core).
Axes of the slice: x: 2, y: 2, z: 4, core: 2. Of those that a mesh axis runs over, the one named last changes fastest.
Arguments:
- queries: bfloat16 [8192, 2048], P(('grp', 'mem')), may hold values from -6 to 6
- keys: bfloat16 [8192, 2048], P(('grp', 'mem')), may hold values from -6 to 6
- values: bfloat16 [8192, 2048], P(('grp', 'mem')), may hold values from -6 to 6
- grad_out: bfloat16 [8192, 2048], P(('grp', 'mem')), may hold values from -0.125 to 0.125
- log_decay: float32 [8, 8192], P(None, ('grp', 'mem')), may hold values from -1.6 to 0
Outputs:
- grad_queries: bfloat16 [8192, 2048], P(('grp', 'mem'))
- grad_keys: bfloat16 [8192, 2048], P(('grp', 'mem'))
- grad_values: bfloat16 [8192, 2048], P(('grp', 'mem'))
All inputs are finite; a program needn't handle non-finite values.
Results may differ from a plain program's by a relative error of at most 0.0052.
Values sent between devices are 32-bit elements; how exact they have to be, the bound alone decides.
A program may use at most 128 MiB of HBM per device.

v0:
```python
import jax
import jax.numpy as jnp
from jax import lax
from jax.sharding import PartitionSpec as P

HEAD_COUNT = 8
DK = 256
DV = 256
BLOCK = 128


def prefix(value, axis, join, neutral, backward):
    count, mine = (lax.axis_size(axis), lax.axis_index(axis))
    pieces = jax.tree.map(lambda part: lax.all_gather(part, axis), value)
    if backward:
        pieces = jax.tree.map(lambda part: part[::-1], pieces)
        mine = count - 1 - mine
    total = jax.tree.map(
        lambda part, zero: jnp.full_like(part, 0) + jnp.asarray(zero, part.dtype), value, neutral
    )

    def turn(position, total):
        longer = join(total, jax.tree.map(lambda part: part[position], pieces))
        return jax.tree.map(lambda new, old: jnp.where(position < mine, new, old), longer, total)

    return lax.fori_loop(0, count - 1, turn, total)


def chain(earlier, later):
    early_decay, early_state = earlier
    late_decay, late_state = later
    return (early_decay * late_decay, late_state + late_decay[:, None, None] * early_state)


def body(queries, keys, values, grad_out, log_decay):
    tokens = queries.shape[0]
    count = tokens // BLOCK
    scale = DK ** (-0.5)
    query_blocks = queries.reshape(count, BLOCK, HEAD_COUNT, DK)
    key_blocks = keys.reshape(count, BLOCK, HEAD_COUNT, DK)
    value_blocks = values.reshape(count, BLOCK, HEAD_COUNT, DV)
    grad_blocks = grad_out.reshape(count, BLOCK, HEAD_COUNT, DV)
    logs = jnp.transpose(log_decay.reshape(HEAD_COUNT, count, BLOCK), (1, 0, 2))
    cumul = jnp.cumsum(logs, axis=2)
    ends = cumul[:, :, -1]
    lower = jnp.tril(jnp.ones((BLOCK, BLOCK), dtype=bool))
    spread = cumul[:, :, :, None] - cumul[:, :, None, :]
    decay = jnp.where(lower, jnp.exp(jnp.where(lower, spread, 0.0)), 0.0)
    scores = jnp.einsum(
        "bthe,bshe->bhts", grad_blocks, value_blocks, preferred_element_type=jnp.float32
    )
    weight_grad = (scores * decay).astype(jnp.bfloat16)
    attend = jnp.einsum(
        "bthd,bshd->bhts", query_blocks, key_blocks, preferred_element_type=jnp.float32
    )
    weight_value = (attend * decay).astype(jnp.bfloat16)
    inner_query = jnp.einsum(
        "bhts,bshd->bthd", weight_grad, key_blocks, preferred_element_type=jnp.float32
    )
    inner_key = jnp.einsum(
        "bhts,bthd->bshd", weight_grad, query_blocks, preferred_element_type=jnp.float32
    )
    inner_value = jnp.einsum(
        "bhts,bthe->bshe", weight_value, grad_blocks, preferred_element_type=jnp.float32
    )
    head_factor = jnp.exp(jnp.transpose(cumul, (0, 2, 1)))[..., None]
    tail_factor = jnp.exp(jnp.transpose(ends[:, :, None] - cumul, (0, 2, 1)))[..., None]
    keys_decayed = (key_blocks * tail_factor).astype(jnp.bfloat16)
    queries_decayed = (query_blocks * head_factor).astype(jnp.bfloat16)
    forward_parts = jnp.einsum(
        "bshd,bshe->bhde", keys_decayed, value_blocks, preferred_element_type=jnp.float32
    )
    reverse_parts = jnp.einsum(
        "bthd,bthe->bhde", queries_decayed, grad_blocks, preferred_element_type=jnp.float32
    )
    block_decay = jnp.exp(ends)
    running = jnp.zeros((HEAD_COUNT, DK, DV), jnp.float32)
    carried = jnp.ones((HEAD_COUNT,), jnp.float32)
    prefix_list = []
    carried_list = []
    for position in range(count):
        prefix_list.append(running)
        carried_list.append(carried)
        running = block_decay[position][:, None, None] * running + forward_parts[position]
        carried = carried * block_decay[position]
    forward_total = running
    running = jnp.zeros((HEAD_COUNT, DK, DV), jnp.float32)
    after = jnp.ones((HEAD_COUNT,), jnp.float32)
    suffix_list = [None] * count
    after_list = [None] * count
    for position in reversed(range(count)):
        suffix_list[position] = running
        after_list[position] = after
        running = block_decay[position][:, None, None] * running + reverse_parts[position]
        after = after * block_decay[position]
    members = lax.axis_size("mem")
    decay_cols = jnp.broadcast_to(carried[None, :, None, None], (1, HEAD_COUNT, members, 1))
    pieces = (
        lax.all_to_all(decay_cols, "mem", split_axis=2, concat_axis=0, tiled=True),
        lax.all_to_all(forward_total[None], "mem", split_axis=2, concat_axis=0, tiled=True),
        lax.all_to_all(running[None], "mem", split_axis=2, concat_axis=0, tiled=True),
    )
    member_decays = pieces[0][:, :, 0, 0]
    width = DK // members
    share_identity = (
        jnp.ones((HEAD_COUNT,), jnp.float32),
        jnp.zeros((HEAD_COUNT, width, DV), jnp.float32),
    )
    forward_prefix = []
    accum = share_identity
    for index in range(members):
        forward_prefix.append(accum)
        accum = chain(accum, (member_decays[index], pieces[1][index]))
    forward_whole = accum
    reverse_prefix = [None] * members
    accum = share_identity
    for index in reversed(range(members)):
        reverse_prefix[index] = accum
        accum = chain(accum, (member_decays[index], pieces[2][index]))
    group_first = prefix(forward_whole, "grp", chain, share_identity, False)
    group_second = prefix(accum, "grp", chain, share_identity, True)
    first_stack = jnp.stack(
        [chain(group_first, forward_prefix[index])[1] for index in range(members)]
    )
    second_stack = jnp.stack(
        [chain(group_second, reverse_prefix[index])[1] for index in range(members)]
    )
    returned = (
        lax.all_to_all(first_stack, "mem", split_axis=0, concat_axis=2, tiled=True),
        lax.all_to_all(second_stack, "mem", split_axis=0, concat_axis=2, tiled=True),
    )
    state_from = returned[0][0]
    grads_from = returned[1][0]
    states_low = (
        jnp.stack(prefix_list) + jnp.stack(carried_list)[:, :, None, None] * state_from[None]
    ).astype(jnp.bfloat16)
    grads_low = (
        jnp.stack(suffix_list) + jnp.stack(after_list)[:, :, None, None] * grads_from[None]
    ).astype(jnp.bfloat16)
    outer_query = jnp.einsum(
        "bthe,bhde->bthd", grad_blocks, states_low, preferred_element_type=jnp.float32
    )
    outer_key = jnp.einsum(
        "bshe,bhde->bshd", value_blocks, grads_low, preferred_element_type=jnp.float32
    )
    outer_value = jnp.einsum(
        "bshd,bhde->bshe", key_blocks, grads_low, preferred_element_type=jnp.float32
    )
    grad_queries = (scale * (inner_query + head_factor * outer_query)).astype(jnp.bfloat16)
    grad_keys = (scale * (inner_key + tail_factor * outer_key)).astype(jnp.bfloat16)
    grad_values = (scale * (inner_value + tail_factor * outer_value)).astype(jnp.bfloat16)
    return (
        grad_queries.reshape(tokens, HEAD_COUNT * DK),
        grad_keys.reshape(tokens, HEAD_COUNT * DK),
        grad_values.reshape(tokens, HEAD_COUNT * DV),
    )


def solution(mesh):
    placed = (
        P(("grp", "mem"), None),
        P(("grp", "mem"), None),
        P(("grp", "mem"), None),
        P(("grp", "mem"), None),
        P(None, ("grp", "mem")),
    )
    return jax.shard_map(
        body,
        mesh=mesh,
        in_specs=placed,
        out_specs=(P(("grp", "mem"), None), P(("grp", "mem"), None), P(("grp", "mem"), None)),
        check_vma=False,
    )
```

profile of v0, /device:TPU:0, one launch (start us, length us, event | category | flops | bytes accessed | tf_op | source)
XLA Modules:
  0.0 301.0 jit_solution(9682326019785282810)
XLA Ops:
  9.3 4.2 %all-to-all-start.1 = ((f32[1,8,4,1]{1,3,0,2:T(1,128)}), f32[1,8,4,1]{1,3,0,2:T(1,128)S(1)}, u32[]{:S(2)}, u32[]{:S(2)}) async-start(f32[1,8,4,1]{1,3,0,2:T(1,128)} %broadcast_in_dim.21), calls=%async_computation.1 | async-start | bytes 4096 | tf_op jit(solution)/shard_map/all_to_all | solution.py:99
  13.6 1.6 copy.135
  20.3 2.9 slice_add_fusion
  23.2 2.6 copy.103
  25.8 4.5 %all-to-all-start.3 = ((f32[1,8,256,256]{3,1,0,2:T(8,128)}), f32[1,8,256,256]{3,1,0,2:T(8,128)}, u32[]{:S(2)}, u32[]{:S(2)}) async-start(f32[1,8,256,256]{3,1,0,2:T(8,128)} %copy.103), calls=%async_computation.3 | async-start | bytes 4194304 | tf_op jit(solution)/shard_map/all_to_all | solution.py:101
  30.3 4.1 %copy.89 = f32[1,8,256,256]{3,1,0,2:T(8,128)} copy(f32[1,8,256,256]{3,2,1,0:T(8,128)} %get-tuple-element.284) | data formatting | bytes 4194304 | tf_op jit(solution)/shard_map/add | solution.py:84
  34.4 21.6 %all-to-all-done.3 = f32[1,8,256,256]{3,1,0,2:T(8,128)} async-done(((f32[1,8,256,256]{3,1,0,2:T(8,128)}), f32[1,8,256,256]{3,1,0,2:T(8,128)}, u32[]{:S(2)}, u32[]{:S(2)}) %all-to-all-start.3) | async-done | bytes 2097184 | tf_op jit(solution)/shard_map/all_to_all | solution.py:101
  56.0 4.4 %all-to-all-start = ((f32[1,8,256,256]{3,1,0,2:T(8,128)}), f32[1,8,256,256]{3,1,0,2:T(8,128)}, u32[]{:S(2)}, u32[]{:S(2)}) async-start(f32[1,8,256,256]{3,1,0,2:T(8,128)} %copy.89), calls=%async_computation | async-start | bytes 4194304 | tf_op jit(solution)/shard_map/all_to_all | solution.py:100
  60.5 3.6 %copy.173 = f32[1,8,4,64,256]{4,3,1,0,2:T(8,128)} copy(f32[1,8,4,64,256]{4,1,3,2,0:T(8,128)} %bitcast.39) | data formatting | bytes 4194304 | tf_op jit(solution)/shard_map/all_to_all | solution.py:101
  64.1 22.1 %all-to-all-done = f32[1,8,256,256]{3,1,0,2:T(8,128)} async-done(((f32[1,8,256,256]{3,1,0,2:T(8,128)}), f32[1,8,256,256]{3,1,0,2:T(8,128)}, u32[]{:S(2)}, u32[]{:S(2)}) %all-to-all-start) | async-done | bytes 2097184 | tf_op jit(solution)/shard_map/all_to_all | solution.py:100
  86.2 2.4 copy.90
  88.6 1.7 fusion.38
  91.1 21.7 %all-gather.1 = f32[8,1,8]{2,1,0:T(1,128)S(1)} all-gather(f32[1,1,8]{2,1,0:T(1,128)S(1)} %get-tuple-element.269), channel_id=1, replica_groups=mesh['grp'=8,'mem'=4] {'grp'}, dimensions={0}, use_global_device_ids=true | all-gather | bytes 288 | tf_op jit(solution)/shard_map/all_gather | solution.py:14
  112.8 16.6 %all-gather = f32[8,1,8]{2,1,0:T(1,128)S(1)} all-gather(f32[1,1,8]{2,1,0:T(1,128)S(1)} %get-tuple-element.270), channel_id=1, replica_groups=mesh['grp'=8,'mem'=4] {'grp'}, dimensions={0}, use_global_device_ids=true | all-gather | bytes 288 | tf_op jit(solution)/shard_map/all_gather | solution.py:14
  129.4 34.7 %all-gather.7.cloned.1.call-done = f32[8,8,64,256]{3,2,1,0:T(8,128)} async-done(((f32[1,8,64,256]{3,2,1,0:T(8,128)}), f32[8,8,64,256]{3,2,1,0:T(8,128)}) %all-gather.7.cloned.1.call-update) | async-done | bytes 4194320 | tf_op jit(solution)/shard_map/all_gather | solution.py:14
  164.1 4.7 %rev.6 = f32[8,8,64,256]{3,2,1,0:T(8,128)} reverse(f32[8,8,64,256]{3,2,1,0:T(8,128)} %all-gather.7.cloned.1.call-done), dimensions={0} | reverse | bytes 8388608 | tf_op jit(solution)/shard_map/rev | solution.py:16
  168.8 8.5 %while.29 = (s32[]{:T(128)}, f32[8,64,256]{2,1,0:T(8,128)S(1)}, s32[]{:T(128)}, f32[8,8,64,256]{3,2,1,0:T(8,128)}, f32[8,8]{1,0:T(8,128)S(1)}, /*index=5*/s32[]{:T(128)}, s32[]{:T(128)}) while((s32[]{:T(128)}, f32[8,64,256]{2,1,0:T(8,128)S(1)}, s32[]{:T(128)}, f32[8,8,64,256]{3,2,1,0:T(8,128)}, f32[8,8]{1,0:T(8,128)S(1)}, ...), condition=%wide.region_4.5_spmd.clone, body=%wide.region_3.4_spmd.clone.sunk | while | flops 524292 | bytes 1573073 | solution.py:26
  177.4 1.7 fusion.51
  179.1 1.6 pad_maximum_fusion.1
  180.6 4.4 %all-to-all-start.4 = ((f32[4,8,64,256]{3,2,1,0:T(8,128)}), f32[4,8,64,256]{3,2,1,0:T(8,128)}, u32[]{:S(2)}, u32[]{:S(2)}) async-start(f32[4,8,64,256]{3,2,1,0:T(8,128)} %pad_maximum_fusion.1), calls=%async_computation.4 | async-start | bytes 4194304 | tf_op jit(solution)/shard_map/all_to_all | solution.py:130
  185.1 52.5 %all-gather.5.cloned.1.call-done = f32[8,8,64,256]{3,2,1,0:T(8,128)} async-done(((f32[1,8,64,256]{3,2,1,0:T(8,128)}), f32[8,8,64,256]{3,2,1,0:T(8,128)}) %all-gather.5.cloned.1.call-update) | async-done | bytes 4194320 | tf_op jit(solution)/shard_map/all_gather | solution.py:14
  237.6 8.5 %while.28 = (s32[]{:T(128)}, f32[8,64,256]{2,1,0:T(8,128)S(1)}, s32[]{:T(128)}, f32[8,8,64,256]{3,2,1,0:T(8,128)}, f32[8,8]{1,0:T(8,128)S(1)}, /*index=5*/s32[]{:T(128)}, s32[]{:T(128)}) while((s32[]{:T(128)}, f32[8,64,256]{2,1,0:T(8,128)S(1)}, s32[]{:T(128)}, f32[8,8,64,256]{3,2,1,0:T(8,128)}, f32[8,8]{1,0:T(8,128)S(1)}, ...), condition=%wide.region_2.3_spmd.clone, body=%wide.region_1.2_spmd.clone.sunk | while | flops 524292 | bytes 1573073 | solution.py:26
  246.1 1.7 add_bitcast_fusion.2
  249.3 4.8 %all-to-all-start.2 = ((f32[4,8,64,256]{3,2,1,0:T(8,128)}), f32[4,8,64,256]{3,2,1,0:T(8,128)}, u32[]{:S(2)}, u32[]{:S(2)}) async-start(f32[4,8,64,256]{3,2,1,0:T(8,128)} %pad_maximum_fusion), calls=%async_computation.2 | async-start | bytes 4194304 | tf_op jit(solution)/shard_map/all_to_all | solution.py:129
  254.1 2.7 fusion.14
  256.8 1.8 copy.106
  258.7 2.3 fusion.24
  261.0 2.1 fusion.28
  263.1 16.5 %all-to-all-done.2 = f32[4,8,64,256]{3,2,1,0:T(8,128)} async-done(((f32[4,8,64,256]{3,2,1,0:T(8,128)}), f32[4,8,64,256]{3,2,1,0:T(8,128)}, u32[]{:S(2)}, u32[]{:S(2)}) %all-to-all-start.2) | async-done | bytes 2097184 | tf_op jit(solution)/shard_map/all_to_all | solution.py:129
  279.6 1.9 copy.94
  287.9 3.2 %fusion.5 = bf16[2,128,8,256]{3,1,2,0:T(8,128)(2,1)} fusion(f32[2,8,256,128]{2,3,1,0:T(8,128)} %fusion.28, f32[2,128,8]{1,2,0:T(8,128)S(1)} %get-tuple-element.264, bf16[2,128,8,256]{3,2,1,0:T(8,128)(2,1)S(1)} %bitcast.295, bf16[2,128,8,256]{3,2,1,0:T(8,128)(2,1)S(1)} %bitcast.288, bf16[2,128,8,256]{3,2,1,0:T(8,128)(2,1)S(1)} %bitcast.299, ...), kind=kOutput, calls=%fused_computation.18 | convolution fusion | flops 271843328 | bytes 6324224 | tf_op jit(solution)/shard_map/bhts,bthe->bshe/dot_general | solution.py:63
  291.1 1.8 copy.117
  (98 shorter events, 33.8 us)
Async XLA Ops:
  7.2 8.1 %copy-start.14 = (bf16[256,2048]{1,0:T(8,128)(2,1)S(1)}, bf16[256,2048]{1,0:T(8,128)(2,1)}, u32[]{:S(2)}) copy-start(bf16[256,2048]{1,0:T(8,128)(2,1)} %param.12) | copy-start | bytes 3145732
  9.3 16.5 %all-to-all-start.1 = ((f32[1,8,4,1]{1,3,0,2:T(1,128)}), f32[1,8,4,1]{1,3,0,2:T(1,128)S(1)}, u32[]{:S(2)}, u32[]{:S(2)}) async-start(f32[1,8,4,1]{1,3,0,2:T(1,128)} %broadcast_in_dim.21), calls=%async_computation.1 | async-start | bytes 4096 | tf_op jit(solution)/shard_map/all_to_all | solution.py:99
  13.6 2.0 copy-start.15
  15.2 2.4 copy-start.4
  15.2 2.0 copy-start.16
  15.6 2.0 copy-start.6
  15.9 3.1 %copy-start.9 = (bf16[32,8,8,256]{3,2,1,0:T(8,128)(2,1)}, bf16[32,8,8,256]{3,2,1,0:T(8,128)(2,1)S(1)}, u32[]{:S(2)}) copy-start(bf16[32,8,8,256]{3,2,1,0:T(8,128)(2,1)S(1)} %copy.132) | copy-start | bytes 3145732
  17.6 1.4 copy-start
  25.8 30.2 %all-to-all-start.3 = ((f32[1,8,256,256]{3,1,0,2:T(8,128)}), f32[1,8,256,256]{3,1,0,2:T(8,128)}, u32[]{:S(2)}, u32[]{:S(2)}) async-start(f32[1,8,256,256]{3,1,0,2:T(8,128)} %copy.103), calls=%async_computation.3 | async-start | bytes 4194304 | tf_op jit(solution)/shard_map/all_to_all | solution.py:101
  56.0 30.2 %all-to-all-start = ((f32[1,8,256,256]{3,1,0,2:T(8,128)}), f32[1,8,256,256]{3,1,0,2:T(8,128)}, u32[]{:S(2)}, u32[]{:S(2)}) async-start(f32[1,8,256,256]{3,1,0,2:T(8,128)} %copy.89), calls=%async_computation | async-start | bytes 4194304 | tf_op jit(solution)/shard_map/all_to_all | solution.py:100
  60.4 103.7 %all-gather.7.cloned.1.call-start = ((), (), s32[]{:S(2)}) async-start(), calls=%async_computation.6 | async-start | bytes 4718592 | tf_op jit(solution)/shard_map/all_gather | solution.py:14
  86.2 2.4 copy-start.3
  88.6 1.7 copy-start.2
  90.3 147.3 %all-gather.5.cloned.1.call-start = ((), (), s32[]{:S(2)}) async-start(), calls=%async_computation.5 | async-start | bytes 4718592 | tf_op jit(solution)/shard_map/all_gather | solution.py:14
  180.6 68.7 %all-to-all-start.4 = ((f32[4,8,64,256]{3,2,1,0:T(8,128)}), f32[4,8,64,256]{3,2,1,0:T(8,128)}, u32[]{:S(2)}, u32[]{:S(2)}) async-start(f32[4,8,64,256]{3,2,1,0:T(8,128)} %pad_maximum_fusion.1), calls=%async_computation.4 | async-start | bytes 4194304 | tf_op jit(solution)/shard_map/all_to_all | solution.py:130
  249.3 4.8 %copy-start.7 = (bf16[32,8,8,256]{3,2,1,0:T(8,128)(2,1)S(1)}, bf16[32,8,8,256]{3,2,1,0:T(8,128)(2,1)}, u32[]{:S(2)}) copy-start(bf16[32,8,8,256]{3,2,1,0:T(8,128)(2,1)} %copy-done.6) | copy-start | bytes 3145732
  249.3 30.3 %all-to-all-start.2 = ((f32[4,8,64,256]{3,2,1,0:T(8,128)}), f32[4,8,64,256]{3,2,1,0:T(8,128)}, u32[]{:S(2)}, u32[]{:S(2)}) async-start(f32[4,8,64,256]{3,2,1,0:T(8,128)} %pad_maximum_fusion), calls=%async_computation.2 | async-start | bytes 4194304 | tf_op jit(solution)/shard_map/all_to_all | solution.py:129
  256.8 1.9 copy-start.10
  258.7 2.3 copy-start.1
  263.1 18.4 %copy-start.8 = (bf16[32,8,8,256]{3,2,1,0:T(8,128)(2,1)S(1)}, bf16[32,8,8,256]{3,2,1,0:T(8,128)(2,1)}, u32[]{:S(2)}) copy-start(bf16[32,8,8,256]{3,2,1,0:T(8,128)(2,1)} %copy-done.6) | copy-start | bytes 3145732
  279.6 2.2 copy-start.11
  281.8 1.0 copy-start.13
  283.4 1.9 copy-start.5
  283.4 1.9 copy-start.12
Sparse Core Ops, SparseCore 0:
  90.4 73.6 all-gather.6
  166.2 71.3 all-gather.4
where the time goes:
time: 303 us; the launch traced here: 301 us
  waiting for transfers between devices  148 us (49%)
  blocking collectives  38.3 us (13%)
  local copies, waits for them, and re-layouts  33.3 us (11%)
  other arithmetic  28.9 us (10%)
  starting transfers between devices  22.4 us (7%)
  matrix products  15 us (5%)
  between operations  14.4 us (5%)
    all_gather x2, waiting for transfers between devices, prefix(): pieces = jax.tree.map(lambda part: lax.all_gather(part, axis), value)  87.2 us
    all_gather x2, blocking collectives, prefix(): pieces = jax.tree.map(lambda part: lax.all_gather(part, axis), value)  38.3 us
    all_to_all x1, waiting for transfers between devices, body(): lax.all_to_all(forward_total[None], 'mem', split_axis=2, concat_axis=0, t...  22.1 us
    all_to_all x1, waiting for transfers between devices, body(): lax.all_to_all(running[None], 'mem', split_axis=2, concat_axis=0, tiled=T...  21.6 us
    all_to_all x1, waiting for transfers between devices, body(): lax.all_to_all(first_stack, 'mem', split_axis=0, concat_axis=2, tiled=True)  16.5 us
    select_n x14, other arithmetic, turn(): jnp.where(position < mine, new, old)  16.5 us
    unnamed x41, local copies, waits for them, and re-layouts  8.32 us
  transfers between devices with their start and end apart: 7, of which 5 were waited for; matrix products, arithmetic and copies ran while one was open for 18% of the time, Pallas kernels for 0%

commit v1 on v0

--- a/solution.py
+++ b/solution.py
@@ -125,8 +125,20 @@
     second_stack = jnp.stack(
         [chain(group_second, reverse_prefix[index])[1] for index in range(members)]
     )
+
+    def see_orders_on_mesh(z_in):
+        return jnp.concatenate(
+            lax.all_to_all(
+                jnp.stack(jnp.split(z_in, lax.axis_size("mem"), 0), 0),
+                axis_name="mem",
+                concat_axis=0,
+                split_axis=0,
+            ),
+            2,
+        )
+
     returned = (
-        lax.all_to_all(first_stack, "mem", split_axis=0, concat_axis=2, tiled=True),
+        see_orders_on_mesh(first_stack),
         lax.all_to_all(second_stack, "mem", split_axis=0, concat_axis=2, tiled=True),
     )
     state_from = returned[0][0]

time: 303 us -> 303 us (level)
  no operation moved by 1% of the time
where the time goes in v1:
time: 303 us; the launch traced here: 301 us
  waiting for transfers between devices  148 us (49%)
  blocking collectives  38.3 us (13%)
  local copies, waits for them, and re-layouts  33.3 us (11%)
  other arithmetic  28.9 us (10%)
  starting transfers between devices  22.4 us (7%)
  matrix products  15 us (5%)
  between operations  14.4 us (5%)
    all_gather x2, waiting for transfers between devices, prefix(): pieces = jax.tree.map(lambda part: lax.all_gather(part, axis), value)  87.2 us
    all_gather x2, blocking collectives, prefix(): pieces = jax.tree.map(lambda part: lax.all_gather(part, axis), value)  38.3 us
    all_to_all x1, waiting for transfers between devices, body(): lax.all_to_all(forward_total[None], 'mem', split_axis=2, concat_axis=0, t...  22.1 us
    all_to_all x1, waiting for transfers between devices, body(): lax.all_to_all(running[None], 'mem', split_axis=2, concat_axis=0, tiled=T...  21.6 us
    all_to_all x1, waiting for transfers between devices, see_orders_on_mesh(): lax.all_to_all(jnp.stack(jnp.split(z_in, lax.axis_size('mem'), 0), 0), ax...  16.5 us
    select_n x14, other arithmetic, turn(): jnp.where(position < mine, new, old)  16.5 us
    unnamed x41, local copies, waits for them, and re-layouts  8.32 us
  transfers between devices with their start and end apart: 7, of which 5 were waited for; matrix products, arithmetic and copies ran while one was open for 18% of the time, Pallas kernels for 0%

profile of v1, /device:TPU:0, one launch (start us, length us, event | category | flops | bytes accessed | tf_op | source)
XLA Modules:
  0.0 301.0 jit_solution(9682326019785282810)
XLA Ops:
  9.3 4.2 %all-to-all-start.1 = ((f32[1,8,4,1]{1,3,0,2:T(1,128)}), f32[1,8,4,1]{1,3,0,2:T(1,128)S(1)}, u32[]{:S(2)}, u32[]{:S(2)}) async-start(f32[1,8,4,1]{1,3,0,2:T(1,128)} %broadcast_in_dim.21), calls=%async_computation.1 | async-start | bytes 4096 | tf_op jit(solution)/shard_map/all_to_all | solution.py:99
  13.6 1.6 copy.135
  20.3 2.9 slice_add_fusion
  23.2 2.6 copy.103
  25.8 4.5 %all-to-all-start.3 = ((f32[1,8,256,256]{3,1,0,2:T(8,128)}), f32[1,8,256,256]{3,1,0,2:T(8,128)}, u32[]{:S(2)}, u32[]{:S(2)}) async-start(f32[1,8,256,256]{3,1,0,2:T(8,128)} %copy.103), calls=%async_computation.3 | async-start | bytes 4194304 | tf_op jit(solution)/shard_map/all_to_all | solution.py:101
  30.3 4.1 %copy.89 = f32[1,8,256,256]{3,1,0,2:T(8,128)} copy(f32[1,8,256,256]{3,2,1,0:T(8,128)} %get-tuple-element.284) | data formatting | bytes 4194304 | tf_op jit(solution)/shard_map/add | solution.py:84
  34.4 21.6 %all-to-all-done.3 = f32[1,8,256,256]{3,1,0,2:T(8,128)} async-done(((f32[1,8,256,256]{3,1,0,2:T(8,128)}), f32[1,8,256,256]{3,1,0,2:T(8,128)}, u32[]{:S(2)}, u32[]{:S(2)}) %all-to-all-start.3) | async-done | bytes 2097184 | tf_op jit(solution)/shard_map/all_to_all | solution.py:101
  56.0 4.4 %all-to-all-start = ((f32[1,8,256,256]{3,1,0,2:T(8,128)}), f32[1,8,256,256]{3,1,0,2:T(8,128)}, u32[]{:S(2)}, u32[]{:S(2)}) async-start(f32[1,8,256,256]{3,1,0,2:T(8,128)} %copy.89), calls=%async_computation | async-start | bytes 4194304 | tf_op jit(solution)/shard_map/all_to_all | solution.py:100
  60.5 3.6 %copy.173 = f32[1,8,4,64,256]{4,3,1,0,2:T(8,128)} copy(f32[1,8,4,64,256]{4,1,3,2,0:T(8,128)} %bitcast.38) | data formatting | bytes 4194304 | tf_op jit(solution)/shard_map/all_to_all | solution.py:101
  64.1 22.1 %all-to-all-done = f32[1,8,256,256]{3,1,0,2:T(8,128)} async-done(((f32[1,8,256,256]{3,1,0,2:T(8,128)}), f32[1,8,256,256]{3,1,0,2:T(8,128)}, u32[]{:S(2)}, u32[]{:S(2)}) %all-to-all-start) | async-done | bytes 2097184 | tf_op jit(solution)/shard_map/all_to_all | solution.py:100
  86.2 2.4 copy.90
  88.6 1.7 fusion.38
  91.1 21.7 %all-gather.1 = f32[8,1,8]{2,1,0:T(1,128)S(1)} all-gather(f32[1,1,8]{2,1,0:T(1,128)S(1)} %get-tuple-element.269), channel_id=1, replica_groups=mesh['grp'=8,'mem'=4] {'grp'}, dimensions={0}, use_global_device_ids=true | all-gather | bytes 288 | tf_op jit(solution)/shard_map/all_gather | solution.py:14
  112.8 16.6 %all-gather = f32[8,1,8]{2,1,0:T(1,128)S(1)} all-gather(f32[1,1,8]{2,1,0:T(1,128)S(1)} %get-tuple-element.270), channel_id=1, replica_groups=mesh['grp'=8,'mem'=4] {'grp'}, dimensions={0}, use_global_device_ids=true | all-gather | bytes 288 | tf_op jit(solution)/shard_map/all_gather | solution.py:14
  129.4 34.7 %all-gather.7.cloned.1.call-done = f32[8,8,64,256]{3,2,1,0:T(8,128)} async-done(((f32[1,8,64,256]{3,2,1,0:T(8,128)}), f32[8,8,64,256]{3,2,1,0:T(8,128)}) %all-gather.7.cloned.1.call-update) | async-done | bytes 4194320 | tf_op jit(solution)/shard_map/all_gather | solution.py:14
  164.1 4.7 %rev.6 = f32[8,8,64,256]{3,2,1,0:T(8,128)} reverse(f32[8,8,64,256]{3,2,1,0:T(8,128)} %all-gather.7.cloned.1.call-done), dimensions={0} | reverse | bytes 8388608 | tf_op jit(solution)/shard_map/rev | solution.py:16
  168.8 8.5 %while.29 = (s32[]{:T(128)}, f32[8,64,256]{2,1,0:T(8,128)S(1)}, s32[]{:T(128)}, f32[8,8,64,256]{3,2,1,0:T(8,128)}, f32[8,8]{1,0:T(8,128)S(1)}, /*index=5*/s32[]{:T(128)}, s32[]{:T(128)}) while((s32[]{:T(128)}, f32[8,64,256]{2,1,0:T(8,128)S(1)}, s32[]{:T(128)}, f32[8,8,64,256]{3,2,1,0:T(8,128)}, f32[8,8]{1,0:T(8,128)S(1)}, ...), condition=%wide.region_4.5_spmd.clone, body=%wide.region_3.4_spmd.clone.sunk | while | flops 524292 | bytes 1573073 | solution.py:26
  177.4 1.7 fusion.51
  179.1 1.6 pad_maximum_fusion.1
  180.6 4.4 %all-to-all-start.4 = ((f32[4,8,64,256]{3,2,1,0:T(8,128)}), f32[4,8,64,256]{3,2,1,0:T(8,128)}, u32[]{:S(2)}, u32[]{:S(2)}) async-start(f32[4,8,64,256]{3,2,1,0:T(8,128)} %pad_maximum_fusion.1), calls=%async_computation.4 | async-start | bytes 4194304 | tf_op jit(solution)/shard_map/all_to_all | solution.py:142
  185.1 52.5 %all-gather.5.cloned.1.call-done = f32[8,8,64,256]{3,2,1,0:T(8,128)} async-done(((f32[1,8,64,256]{3,2,1,0:T(8,128)}), f32[8,8,64,256]{3,2,1,0:T(8,128)}) %all-gather.5.cloned.1.call-update) | async-done | bytes 4194320 | tf_op jit(solution)/shard_map/all_gather | solution.py:14
  237.6 8.5 %while.28 = (s32[]{:T(128)}, f32[8,64,256]{2,1,0:T(8,128)S(1)}, s32[]{:T(128)}, f32[8,8,64,256]{3,2,1,0:T(8,128)}, f32[8,8]{1,0:T(8,128)S(1)}, /*index=5*/s32[]{:T(128)}, s32[]{:T(128)}) while((s32[]{:T(128)}, f32[8,64,256]{2,1,0:T(8,128)S(1)}, s32[]{:T(128)}, f32[8,8,64,256]{3,2,1,0:T(8,128)}, f32[8,8]{1,0:T(8,128)S(1)}, ...), condition=%wide.region_2.3_spmd.clone, body=%wide.region_1.2_spmd.clone.sunk | while | flops 524292 | bytes 1573073 | solution.py:26
  246.1 1.7 add_bitcast_fusion.2
  249.3 4.8 %all-to-all-start.2 = ((f32[4,1,8,64,256]{4,3,2,1,0:T(8,128)}), f32[4,1,8,64,256]{4,3,2,1,0:T(8,128)}, u32[]{:S(2)}, u32[]{:S(2)}) async-start(f32[4,1,8,64,256]{4,3,2,1,0:T(8,128)} %pad_maximum_fusion), calls=%async_computation.2 | async-start | bytes 4194304 | tf_op jit(solution)/shard_map/all_to_all | solution.py:131
  254.1 2.7 fusion.14
  256.8 1.8 copy.106
  258.7 2.3 fusion.24
  261.0 2.1 fusion.28
  263.1 16.5 %all-to-all-done.2 = f32[4,1,8,64,256]{4,3,2,1,0:T(8,128)} async-done(((f32[4,1,8,64,256]{4,3,2,1,0:T(8,128)}), f32[4,1,8,64,256]{4,3,2,1,0:T(8,128)}, u32[]{:S(2)}, u32[]{:S(2)}) %all-to-all-start.2) | async-done | bytes 2097184 | tf_op jit(solution)/shard_map/all_to_all | solution.py:131
  279.6 1.9 copy.94
  287.9 3.2 %fusion.5 = bf16[2,128,8,256]{3,1,2,0:T(8,128)(2,1)} fusion(f32[2,8,256,128]{2,3,1,0:T(8,128)} %fusion.28, f32[2,128,8]{1,2,0:T(8,128)S(1)} %get-tuple-element.264, bf16[2,128,8,256]{3,2,1,0:T(8,128)(2,1)S(1)} %bitcast.293, bf16[2,128,8,256]{3,2,1,0:T(8,128)(2,1)S(1)} %bitcast.286, bf16[2,128,8,256]{3,2,1,0:T(8,128)(2,1)S(1)} %bitcast.297, ...), kind=kOutput, calls=%fused_computation.18 | convolution fusion | flops 271843328 | bytes 6324224 | tf_op jit(solution)/shard_map/bhts,bthe->bshe/dot_general | solution.py:63
  291.1 1.8 copy.117
  (98 shorter events, 33.8 us)
Async XLA Ops:
  7.2 8.1 %copy-start.14 = (bf16[256,2048]{1,0:T(8,128)(2,1)S(1)}, bf16[256,2048]{1,0:T(8,128)(2,1)}, u32[]{:S(2)}) copy-start(bf16[256,2048]{1,0:T(8,128)(2,1)} %param.12) | copy-start | bytes 3145732
  9.3 16.5 %all-to-all-start.1 = ((f32[1,8,4,1]{1,3,0,2:T(1,128)}), f32[1,8,4,1]{1,3,0,2:T(1,128)S(1)}, u32[]{:S(2)}, u32[]{:S(2)}) async-start(f32[1,8,4,1]{1,3,0,2:T(1,128)} %broadcast_in_dim.21), calls=%async_computation.1 | async-start | bytes 4096 | tf_op jit(solution)/shard_map/all_to_all | solution.py:99
  13.6 2.0 copy-start.15
  15.2 2.4 copy-start.4
  15.2 2.0 copy-start.16
  15.6 2.0 copy-start.6
  15.9 3.1 %copy-start.9 = (bf16[32,8,8,256]{3,2,1,0:T(8,128)(2,1)}, bf16[32,8,8,256]{3,2,1,0:T(8,128)(2,1)S(1)}, u32[]{:S(2)}) copy-start(bf16[32,8,8,256]{3,2,1,0:T(8,128)(2,1)S(1)} %copy.132) | copy-start | bytes 3145732
  17.6 1.4 copy-start
  25.8 30.2 %all-to-all-start.3 = ((f32[1,8,256,256]{3,1,0,2:T(8,128)}), f32[1,8,256,256]{3,1,0,2:T(8,128)}, u32[]{:S(2)}, u32[]{:S(2)}) async-start(f32[1,8,256,256]{3,1,0,2:T(8,128)} %copy.103), calls=%async_computation.3 | async-start | bytes 4194304 | tf_op jit(solution)/shard_map/all_to_all | solution.py:101
  56.0 30.2 %all-to-all-start = ((f32[1,8,256,256]{3,1,0,2:T(8,128)}), f32[1,8,256,256]{3,1,0,2:T(8,128)}, u32[]{:S(2)}, u32[]{:S(2)}) async-start(f32[1,8,256,256]{3,1,0,2:T(8,128)} %copy.89), calls=%async_computation | async-start | bytes 4194304 | tf_op jit(solution)/shard_map/all_to_all | solution.py:100
  60.4 103.7 %all-gather.7.cloned.1.call-start = ((), (), s32[]{:S(2)}) async-start(), calls=%async_computation.6 | async-start | bytes 4718592 | tf_op jit(solution)/shard_map/all_gather | solution.py:14
  86.2 2.4 copy-start.3
  88.6 1.7 copy-start.2
  90.3 147.3 %all-gather.5.cloned.1.call-start = ((), (), s32[]{:S(2)}) async-start(), calls=%async_computation.5 | async-start | bytes 4718592 | tf_op jit(solution)/shard_map/all_gather | solution.py:14
  180.6 68.7 %all-to-all-start.4 = ((f32[4,8,64,256]{3,2,1,0:T(8,128)}), f32[4,8,64,256]{3,2,1,0:T(8,128)}, u32[]{:S(2)}, u32[]{:S(2)}) async-start(f32[4,8,64,256]{3,2,1,0:T(8,128)} %pad_maximum_fusion.1), calls=%async_computation.4 | async-start | bytes 4194304 | tf_op jit(solution)/shard_map/all_to_all | solution.py:142
  249.3 4.8 %copy-start.7 = (bf16[32,8,8,256]{3,2,1,0:T(8,128)(2,1)S(1)}, bf16[32,8,8,256]{3,2,1,0:T(8,128)(2,1)}, u32[]{:S(2)}) copy-start(bf16[32,8,8,256]{3,2,1,0:T(8,128)(2,1)} %copy-done.6) | copy-start | bytes 3145732
  249.3 30.3 %all-to-all-start.2 = ((f32[4,1,8,64,256]{4,3,2,1,0:T(8,128)}), f32[4,1,8,64,256]{4,3,2,1,0:T(8,128)}, u32[]{:S(2)}, u32[]{:S(2)}) async-start(f32[4,1,8,64,256]{4,3,2,1,0:T(8,128)} %pad_maximum_fusion), calls=%async_computation.2 | async-start | bytes 4194304 | tf_op jit(solution)/shard_map/all_to_all | solution.py:131
  256.8 1.9 copy-start.10
  258.7 2.3 copy-start.1
  263.1 18.4 %copy-start.8 = (bf16[32,8,8,256]{3,2,1,0:T(8,128)(2,1)S(1)}, bf16[32,8,8,256]{3,2,1,0:T(8,128)(2,1)}, u32[]{:S(2)}) copy-start(bf16[32,8,8,256]{3,2,1,0:T(8,128)(2,1)} %copy-done.6) | copy-start | bytes 3145732
  279.6 2.2 copy-start.11
  281.8 1.0 copy-start.13
  283.4 1.9 copy-start.5
  283.4 1.9 copy-start.12
Sparse Core Ops, SparseCore 0:
  90.4 73.6 all-gather.6
  166.2 71.3 all-gather.4
